TPU v7x, 32 devices: a whole 2x2x4 slice. The times are simulated.
32 devices in a mesh: seq: 8 (over y, x, core), head: 4 (over z).
Axes of the slice: x: 2, y: 2, z: 4, core: 2. Of those that a mesh axis runs over, the one named last changes fastest.
Arguments:
- queries: bfloat16 [16384, 512], P('seq', 'head'), may hold values from -6 to 6
- keys: bfloat16 [16384, 512], P('seq', 'head'), may hold values from -6 to 6
- values: bfloat16 [16384, 512], P('seq', 'head'), may hold values from -6 to 6
- level_ids: int32 [16384], P('seq'), may hold values from 0 to 63
- level_table: float32 [64, 15], replicated, may hold values from 0 to 4, as said below
- out_cotangent: bfloat16 [16384, 2048], P('seq', 'head'), may hold values from -6 to 6
Outputs:
- attn_out: bfloat16 [16384, 512], P('seq', 'head')
- weight_grad: float32 [2048, 512], P('seq', 'head')
Inputs may be any that keep to these rules, and one draw needn't show every extreme that they name: `level_table`: positive coefficients.
All inputs are finite; a program needn't handle non-finite values.
Results may differ from a plain program's by a relative error of at most 0.0043.
Values may be sent and summed in bfloat16 or wider, within the bound.
A program may use at most 64 MiB of HBM per device.

v0:
```python
import jax
import jax.numpy as jnp
from jax import lax
from jax.sharding import PartitionSpec as P

EPSILON = 1e-06
HIGHEST = lax.Precision.HIGHEST


def partner_2(value, axis, stride):
    mask = 2**stride
    pairs = [(source, source ^ mask) for source in range(lax.axis_size(axis))]
    return lax.ppermute(value, axis, pairs)


def level_index(row_pos, col_pos, bit_count):
    xor_value = jnp.bitwise_xor(row_pos, col_pos)
    levels = jnp.zeros(xor_value.shape, jnp.int32)
    for shift_by in range(bit_count):
        levels = levels + (jnp.right_shift(xor_value, shift_by) > 0).astype(jnp.int32)
    return levels


def body(queries, keys, values, level_ids, level_table, out_cotangent):
    full_cotangent = lax.all_gather(out_cotangent, "head", axis=1, tiled=True)
    block_len = queries.shape[0]
    head_dim = queries.shape[1]
    local_bits = block_len.bit_length() - 1
    seq_bits = lax.axis_size("seq").bit_length() - 1
    table_rows = level_table.shape[0]
    onehot = (level_ids[:, None] == jnp.arange(table_rows, dtype=jnp.int32)[None, :]).astype(
        jnp.float32
    )
    coeff = jnp.dot(onehot, level_table, precision=HIGHEST, preferred_element_type=jnp.float32)
    state = lax.dot_general(
        keys, values, (((0,), (0,)), ((), ())), preferred_element_type=jnp.float32
    )
    own_index = lax.axis_index("seq")
    subtree = state
    found = []
    for level in range(seq_bits):
        partner = partner_2(subtree, "seq", level)
        upper = jnp.bitwise_and(jnp.right_shift(own_index, level), 1) == 1
        found.append(jnp.where(upper, partner, 0.0))
        subtree = subtree + partner
    sibling = jnp.stack(found)
    flat_states = sibling.transpose(1, 0, 2).reshape(head_dim, seq_bits * head_dim)
    readout = jnp.dot(
        queries.astype(jnp.float32),
        flat_states,
        precision=HIGHEST,
        preferred_element_type=jnp.float32,
    )
    readout = readout.reshape(block_len, seq_bits, head_dim)
    cross = jnp.sum(readout * coeff[:, local_bits + 1 :, None], axis=1)
    rows_per = min(512, block_len)
    pieces = []
    for first in range(0, block_len, rows_per):
        last = first + rows_per
        row_pos = jnp.arange(first, last, dtype=jnp.int32)[:, None]
        col_pos = jnp.arange(last, dtype=jnp.int32)[None, :]
        levels = level_index(row_pos, col_pos, local_bits)
        rows_coeff = coeff[first:last]
        weights = jnp.zeros((rows_per, last), jnp.float32)
        for level in range(local_bits + 1):
            weights = weights + jnp.where(levels == level, rows_coeff[:, level : level + 1], 0.0)
        weights = jnp.where(col_pos <= row_pos, weights, 0.0)
        scores = lax.dot_general(
            queries[first:last],
            keys[:last],
            (((1,), (1,)), ((), ())),
            preferred_element_type=jnp.float32,
        )
        mixed = (weights * scores).astype(jnp.bfloat16)
        pieces.append(jnp.dot(mixed, values[:last], preferred_element_type=jnp.float32))
    local = jnp.concatenate(pieces, axis=0)
    total = local + cross
    normed = total * lax.rsqrt(jnp.mean(total * total, axis=1, keepdims=True) + EPSILON)
    attn_out = normed.astype(jnp.bfloat16)
    scale = (block_len * lax.axis_size("seq")) ** (-0.5)
    weight_grad = lax.psum_scatter(
        lax.dot_general(
            full_cotangent, attn_out, (((0,), (0,)), ((), ())), preferred_element_type=jnp.float32
        )
        * scale,
        "seq",
        scatter_dimension=0,
        tiled=True,
    )
    return (attn_out, weight_grad)


def solution(mesh):
    in_specs = (
        P("seq", "head"),
        P("seq", "head"),
        P("seq", "head"),
        P("seq"),
        P(),
        P("seq", "head"),
    )
    out_specs = (P("seq", "head"), P("seq", "head"))
    return jax.shard_map(body, mesh=mesh, in_specs=in_specs, out_specs=out_specs, check_vma=False)
```

profile of v0, /device:TPU:15, one launch (start us, length us, event | category | flops | bytes accessed | tf_op | source)
XLA Modules:
  0.0 207.6 jit_solution(2706269134878634147)
XLA Ops:
  7.2 0.0 all-gather.2.cloned.1.call-start
  7.3 0.7 all-gather.2.cloned.1.call-update
  8.0 0.0 reduce-scatter.2.cloned.1.call-start
  8.0 1.5 fusion.168
  9.5 0.7 collective-permute-start
  10.3 0.9 fusion.69
  11.4 8.8 %fusion.4 = f32[512,128]{1,0:T(8,128)S(1)} fusion(f32[512]{0:T(512)S(1)} %bitcast.99, f32[512]{0:T(512)S(1)} %bitcast.100, f32[512]{0:T(512)S(1)} %bitcast.101, f32[512]{0:T(512)S(1)} %bitcast.102, f32[512]{0:T(512)S(1)} %bitcast.103, f32[512]{0:T(512)S(1)} %bitcast.104, f32[512]{0:T(512)S(1)} %bitcast.115, f32[512]{0:T(512)S(1)} %bitcast.116, ...), kind=kOutput, calls=%fused_computation.52 | convolution fusion | flops 467927040 | bytes 1206272 | tf_op jit(solution)/shard_map/dot_general | solution.py:75
  20.2 12.1 %fusion.2 = f32[512,128]{1,0:T(8,128)S(1)} fusion(bf16[2048,128]{1,0:T(8,128)(2,1)S(1)} %copy-done.3, bf16[2048,128]{1,0:T(8,128)(2,1)S(1)} %copy-done.2, f32[512]{0:T(512)S(1)} %bitcast.75, f32[512]{0:T(512)S(1)} %bitcast.76, f32[512]{0:T(512)S(1)} %bitcast.77, f32[512]{0:T(512)S(1)} %bitcast.78, f32[512]{0:T(512)S(1)} %bitcast.79, f32[512]{0:T(512)S(1)} %bitcast.80, ...), kind=kOutput, calls=%fused_computation.50 | convolution fusion | flops 623902720 | bytes 1468416 | tf_op jit(solution)/shard_map/dot_general | solution.py:75
  32.3 6.2 %fusion.5 = f32[512,128]{1,0:T(8,128)S(1)} fusion(f32[512]{0:T(512)S(1)} %bitcast.87, f32[512]{0:T(512)S(1)} %bitcast.88, f32[512]{0:T(512)S(1)} %bitcast.89, f32[512]{0:T(512)S(1)} %bitcast.90, f32[512]{0:T(512)S(1)} %bitcast.91, f32[512]{0:T(512)S(1)} %bitcast.92, f32[512]{0:T(512)S(1)} %bitcast.93, f32[512]{0:T(512)S(1)} %bitcast.94, ...), kind=kOutput, calls=%fused_computation.53 | convolution fusion | flops 311951360 | bytes 944128 | tf_op jit(solution)/shard_map/dot_general | solution.py:75
  38.6 0.3 collective-permute-start.1
  38.9 3.4 %collective-permute-done.1 = f32[128,128]{1,0:T(8,128)S(1)} collective-permute-done((f32[128,128]{1,0:T(8,128)S(1)}, f32[128,128]{1,0:T(8,128)S(1)}, u32[]{:S(2)}, u32[]{:S(2)}) %collective-permute-start.1) | collective-permute-done | bytes 65568 | tf_op jit(solution)/shard_map/ppermute | solution.py:13
  42.4 0.3 collective-permute-start.2
  42.6 2.1 fusion.6
  44.7 0.8 collective-permute-done.2
  45.6 0.1 copy.11
  45.7 1.4 fusion.169
  47.1 0.4 multiply_reduce_fusion
  47.5 0.3 copy.12
  47.8 0.4 multiply_reduce_fusion.1
  48.2 0.3 multiply_convert_fusion.2
  48.6 108.8 %all-gather.2.cloned.1.call-done = bf16[2048,2048]{1,0:T(8,128)(2,1)} async-done(((bf16[2048,512]{1,0:T(8,128)(2,1)}), bf16[2048,2048]{1,0:T(8,128)(2,1)}) %all-gather.2.cloned.1.call-update) | async-done | bytes 8388624 | tf_op jit(solution)/shard_map/all_gather | solution.py:25
  157.4 5.7 %fusion.1 = f32[2048,128]{0,1:T(8,128)} fusion(bf16[2048,128]{1,0:T(8,128)(2,1)S(1)} %multiply_convert_fusion.2, bf16[2048,2048]{1,0:T(8,128)(2,1)} %all-gather.2.cloned.1.call-done), kind=kOutput, calls=%fused_computation.33 | convolution fusion | flops 1074003968 | bytes 9961472 | tf_op jit(solution)/shard_map/dot_general | solution.py:82
  163.2 35.9 %reduce-scatter.2.cloned.1.call-done = f32[256,128]{0,1:T(8,128)} async-done(((f32[2048,128]{0,1:T(8,128)}), f32[256,128]{0,1:T(8,128)}) %reduce-scatter.2.cloned.1.call-update) | async-done | bytes 131088 | tf_op jit(solution)/shard_map/reduce_scatter | solution.py:81
  199.1 1.7 copy.13
  (26 shorter events, 0.2 us)
Async XLA Ops:
  7.2 3.1 %copy-start = (f32[64,15]{0,1:T(8,128)S(1)}, f32[64,15]{0,1:T(8,128)}, u32[]{:S(2)}) copy-start(f32[64,15]{0,1:T(8,128)} %param.10) | copy-start | bytes 11524
  7.2 4.1 %copy-start.2 = (bf16[2048,128]{1,0:T(8,128)(2,1)S(1)}, bf16[2048,128]{1,0:T(8,128)(2,1)}, u32[]{:S(2)}) copy-start(bf16[2048,128]{1,0:T(8,128)(2,1)} %param.7) | copy-start | bytes 1572868
  7.2 4.1 %copy-start.3 = (bf16[2048,128]{1,0:T(8,128)(2,1)S(1)}, bf16[2048,128]{1,0:T(8,128)(2,1)}, u32[]{:S(2)}) copy-start(bf16[2048,128]{1,0:T(8,128)(2,1)} %param.8) | copy-start | bytes 1572868
  7.2 3.1 %copy-start.5 = (s32[2048]{0:T(1024)S(1)}, s32[2048]{0:T(1024)}, u32[]{:S(2)}) copy-start(s32[2048]{0:T(1024)} %param.9) | copy-start | bytes 24580
  7.2 4.1 %copy-start.4 = (bf16[2048,128]{1,0:T(8,128)(2,1)S(1)}, bf16[2048,128]{1,0:T(8,128)(2,1)}, u32[]{:S(2)}) copy-start(bf16[2048,128]{1,0:T(8,128)(2,1)} %param.6) | copy-start | bytes 1572868
  7.2 150.2 %all-gather.2.cloned.1.call-start = ((), (), s32[]{:S(2)}) async-start(), calls=%async_computation.1 | async-start | bytes 10485760 | tf_op jit(solution)/shard_map/all_gather | solution.py:25
  8.0 191.2 %reduce-scatter.2.cloned.1.call-start = ((), (), s32[]{:S(2)}) async-start(), calls=%async_computation.2 | async-start | bytes 1179648 | tf_op jit(solution)/shard_map/reduce_scatter | solution.py:81
  9.5 29.0 %collective-permute-start = (f32[128,128]{1,0:T(8,128)S(1)}, f32[128,128]{1,0:T(8,128)S(1)}, u32[]{:S(2)}, u32[]{:S(2)}) collective-permute-start(f32[128,128]{1,0:T(8,128)S(1)} %fusion.168), channel_id=1, source_target_pairs={{0,4},{4,0},{8,12},{12,8},{16,20},{20,16},{24,28},{28,24},{1,5},{5... | collective-permute-start | bytes 196616 | tf_op jit(solution)/shard_map/ppermute | solution.py:13
  38.6 3.8 %collective-permute-start.1 = (f32[128,128]{1,0:T(8,128)S(1)}, f32[128,128]{1,0:T(8,128)S(1)}, u32[]{:S(2)}, u32[]{:S(2)}) collective-permute-start(f32[128,128]{1,0:T(8,128)S(1)} %get-tuple-element.57), channel_id=1, source_target_pairs={{0,8},{4,12},{8,0},{12,4},{16,24},{20,28},{24,16},{28,20},{1,9},{5... | collective-permute-start | bytes 196616 | tf_op jit(solution)/shard_map/ppermute | solution.py:13
  42.4 3.2 %collective-permute-start.2 = (f32[128,128]{1,0:T(8,128)S(1)}, f32[128,128]{1,0:T(8,128)S(1)}, u32[]{:S(2)}, u32[]{:S(2)}) collective-permute-start(f32[128,128]{1,0:T(8,128)S(1)} %get-tuple-element.59), channel_id=1, source_target_pairs={{0,16},{4,20},{8,24},{12,28},{16,0},{20,4},{24,8},{28,12},{1,17},{... | collective-permute-start | bytes 196616 | tf_op jit(solution)/shard_map/ppermute | solution.py:13
  48.6 114.6 %copy-start.1 = (bf16[2048,128]{1,0:T(8,128)(2,1)}, bf16[2048,128]{1,0:T(8,128)(2,1)S(1)}, u32[]{:S(2)}) copy-start(bf16[2048,128]{1,0:T(8,128)(2,1)S(1)} %multiply_convert_fusion.2) | copy-start | bytes 1572868
Sparse Core Ops, SparseCore 0:
  9.6 147.7 all-gather.1
  163.3 35.7 reduce-scatter.1
where the time goes:
time: 211 us; the launch traced here: 208 us
  waiting for transfers between devices  150 us (71%)
  matrix products  38.8 us (18%)
  between operations  14.3 us (7%)
  local copies, waits for them, and re-layouts  2.23 us (1%)
    all_gather x1, waiting for transfers between devices, body(): full_cotangent = lax.all_gather(out_cotangent, 'head', axis=1, tiled=True)  109 us
    reduce_scatter x1, waiting for transfers between devices, body(): lax.psum_scatter(lax.dot_general(full_cotangent, attn_out, (((0,), (0,)),...  35.9 us
    dot_general x4, matrix products, body(): jnp.dot(mixed, values[:last], preferred_element_type=jnp.float32)  29.2 us
    dot_general x1, matrix products, body(): lax.dot_general(full_cotangent, attn_out, (((0,), (0,)), ((), ())), prefe...  5.74 us
    ppermute x3, waiting for transfers between devices, partner_2(): return lax.ppermute(value, axis, pairs)  4.25 us
  transfers between devices with their start and end apart: 5, of which 4 were waited for; matrix products, arithmetic and copies ran while one was open for 17% of the time, Pallas kernels for 0%

commit v1 on v0

v1 whole, which is shorter than its diff:
```python
import functools

import jax
import jax.numpy as jnp
from jax import lax
from jax.experimental import pallas as pl
from jax.experimental.pallas import tpu as pltpu
from jax.sharding import PartitionSpec as P

EPSILON = 1e-06
TILE = 128
CHUNKS = 4
MESH = pl.DeviceIdType.MESH
F32 = jnp.float32
BF16 = jnp.bfloat16


def dot(a, b, ca, cb):
    return lax.dot_general(a, b, (((ca,), (cb,)), ((), ())), preferred_element_type=F32)


def tile_levels(tile):
    row = lax.broadcasted_iota(jnp.int32, (tile, tile), 0)
    col = lax.broadcasted_iota(jnp.int32, (tile, tile), 1)
    apart = jnp.bitwise_xor(row, col)
    levels = jnp.zeros((tile, tile), jnp.int32)
    for bit in range(tile.bit_length() - 1):
        levels = levels + (jnp.right_shift(apart, bit) > 0).astype(jnp.int32)
    return jnp.where(col <= row, levels, -1)


def kernel(
    n_seq, n_head,
    q_hbm, k_hbm, v_hbm, ids_ref, table_ref, cot_hbm,
    attn_hbm, grad_ref,
    q_ref, k_ref, v_ref, cot_ref, levels_ref, coeff_ref, total_ref, sib_ref,
    state_ref, states_ref, flat_ref, attn_ref, gather_ref, acc_ref,
    share_ref, shares_ref, final_ref, finals_ref,
    load_sem, out_sem, state_send, state_recv, ring_send, ring_recv,
    share_send, share_recv, final_send, final_recv,
):
    seq, head = lax.axis_index("seq"), lax.axis_index("head")
    block_len, head_dim = q_ref.shape
    width = cot_ref.shape[1]
    tiles = block_len // TILE
    chunk = block_len // CHUNKS
    tile_bits = TILE.bit_length() - 1
    local_bits = block_len.bit_length() - 1
    inner = local_bits - tile_bits
    seq_bits = n_seq.bit_length() - 1
    owners = n_seq // n_head
    rows_per = max(16, head_dim // n_seq)
    reducers = head_dim // rows_per
    piece = finals_ref.shape[1]
    scale = (block_len * n_seq) ** (-0.5)

    loads = [
        pltpu.make_async_copy(src, dst, load_sem.at[i])
        for i, (src, dst) in enumerate(
            [(k_hbm, k_ref), (v_hbm, v_ref), (q_hbm, q_ref), (cot_hbm, cot_ref)]
        )
    ]
    for load in loads:
        load.start()

    barrier = pltpu.get_barrier_semaphore()
    me = seq * n_head + head

    def greet(step, carry):
        other = lax.rem(me + step, n_seq * n_head)
        pl.semaphore_signal(
            barrier, inc=1, device_id=(other // n_head, lax.rem(other, n_head)),
            device_id_type=MESH,
        )
        return carry

    lax.fori_loop(1, n_seq * n_head, greet, 0)

    table = table_ref[...]
    high = table.astype(BF16)
    rest = table - high.astype(F32)
    mid = rest.astype(BF16)
    low = (rest - mid.astype(F32)).astype(BF16)
    table3 = jnp.concatenate([high, mid, low], axis=0)
    levels_ref[...] = tile_levels(TILE)

    loads[0].wait()
    loads[1].wait()
    nodes = [
        dot(k_ref[pl.ds(i * TILE, TILE), :], v_ref[pl.ds(i * TILE, TILE), :], 0, 0)
        for i in range(tiles)
    ]
    for bit in range(inner):
        for i in range(tiles):
            place = (i >> bit) ^ 1
            value = nodes[place].astype(BF16) if (i >> bit) & 1 else jnp.zeros((head_dim, head_dim), BF16)
            sib_ref[i, :, pl.ds(bit * head_dim, head_dim)] = value
        nodes = [nodes[2 * i] + nodes[2 * i + 1] for i in range(len(nodes) // 2)]
    state_ref[...] = nodes[0].astype(BF16)

    pl.semaphore_wait(barrier, n_seq * n_head - 1)

    def state_copy(target):
        return pltpu.make_async_remote_copy(
            src_ref=state_ref, dst_ref=states_ref.at[seq],
            send_sem=state_send.at[target], recv_sem=state_recv.at[seq],
            device_id=(target, head), device_id_type=MESH,
        )

    for target in range(1, n_seq):
        @pl.when(seq < target)
        def _():
            state_copy(target).start()

    loads[2].wait()

    def local_tile(i, carry):
        rows = pl.ds(pl.multiple_of(i * TILE, TILE), TILE)
        row_ids = lax.broadcasted_iota(jnp.int32, (table.shape[0], TILE), 0)
        onehot = (row_ids == ids_ref[:, rows]).astype(F32).astype(BF16)
        coeff = dot(jnp.concatenate([onehot] * 3, axis=0), table3, 0, 0)
        coeff_ref[rows, :] = coeff
        levels = levels_ref[...]
        weights = jnp.zeros((TILE, TILE), F32)
        for level in range(tile_bits + 1):
            weights = jnp.where(levels == level, coeff[:, level : level + 1], weights)
        query = q_ref[rows, :]
        scores = dot(query, k_ref[rows, :], 1, 1)
        total = dot((weights * scores).astype(BF16), v_ref[rows, :], 1, 0)
        readout = dot(query, sib_ref[i], 1, 0)
        for bit in range(inner):
            level = tile_bits + 1 + bit
            total += coeff[:, level : level + 1] * readout[:, bit * head_dim : (bit + 1) * head_dim]
        total_ref[rows, :] = total
        return carry

    lax.fori_loop(0, tiles, local_tile, 0, unroll=4)

    for bit in range(seq_bits):
        span = 2**bit
        node = seq // span
        columns = pl.ds(bit * head_dim, head_dim)

        @pl.when(lax.rem(node, 2) == 1)
        def _():
            total = jnp.zeros((head_dim, head_dim), F32)
            for offset in range(span):
                source = (node - 1) * span + offset
                pltpu.make_async_remote_copy(
                    src_ref=state_ref, dst_ref=states_ref.at[source],
                    send_sem=state_send.at[0], recv_sem=state_recv.at[source],
                    device_id=(source, head), device_id_type=MESH,
                ).wait_recv()
                total += states_ref[source].astype(F32)
            upper = total.astype(BF16)
            flat_ref[pl.ds(0, head_dim), columns] = upper
            flat_ref[pl.ds(head_dim, head_dim), columns] = (total - upper.astype(F32)).astype(BF16)

        @pl.when(lax.rem(node, 2) == 0)
        def _():
            flat_ref[:, columns] = jnp.zeros((2 * head_dim, head_dim), BF16)

    right, left = lax.rem(head + 1, n_head), lax.rem(head + n_head - 1, n_head)

    def reach(way, c):
        return n_head // 2 if (c < CHUNKS // 2) == (way == 0) else (n_head - 1) // 2

    def ring_copy(way, distance, c):
        origin = lax.rem(head + (n_head - distance if way == 0 else distance), n_head)
        return pltpu.make_async_remote_copy(
            src_ref=gather_ref.at[origin, c], dst_ref=gather_ref.at[origin, c],
            send_sem=ring_send.at[way, distance, c], recv_sem=ring_recv.at[way, distance, c],
            device_id=(seq, right if way == 0 else left), device_id_type=MESH,
        )

    def ring_arrival(way, distance, c):
        origin = lax.rem(head + (n_head - distance if way == 0 else distance), n_head)
        pltpu.make_async_remote_copy(
            src_ref=gather_ref.at[origin, c], dst_ref=gather_ref.at[origin, c],
            send_sem=ring_send.at[way, distance - 1, c], recv_sem=ring_recv.at[way, distance - 1, c],
            device_id=(seq, right if way == 0 else left), device_id_type=MESH,
        ).wait_recv()
        return origin

    def attn_tile(first):
        def one(i, carry):
            rows = pl.ds(pl.multiple_of(first * chunk + i * TILE, TILE), TILE)
            query = q_ref[rows, :]
            readout = dot(jnp.concatenate([query, query], axis=1), flat_ref[...], 1, 0)
            coeff = coeff_ref[rows, :]
            cross = jnp.zeros((TILE, head_dim), F32)
            for bit in range(seq_bits):
                level = local_bits + 1 + bit
                cross += coeff[:, level : level + 1] * readout[:, bit * head_dim : (bit + 1) * head_dim]
            total = total_ref[rows, :] + cross
            normed = total * lax.rsqrt(jnp.mean(total * total, axis=1, keepdims=True) + EPSILON)
            attn_ref[rows, :] = normed.astype(BF16)
            gather_ref[head, first, :, pl.ds(pl.multiple_of(i * TILE, TILE), TILE)] = normed.T.astype(BF16)
            return carry
        return one

    for c in range(CHUNKS):
        lax.fori_loop(0, chunk // TILE, attn_tile(c), 0, unroll=True)
        for way in range(2):
            if reach(way, c) > 0:
                ring_copy(way, 0, c).start()

    attn_copy = pltpu.make_async_copy(attn_ref, attn_hbm, out_sem.at[0])
    attn_copy.start()

    def multiply(origin, c, fresh):
        part = dot(gather_ref[origin, c], cot_ref[pl.ds(c * chunk, chunk), :], 1, 0)
        if fresh:
            acc_ref[origin] = part
        else:
            acc_ref[origin] += part

    def share_copy(origin, target):
        return pltpu.make_async_remote_copy(
            src_ref=share_ref.at[origin, pl.ds(target * rows_per, rows_per), :],
            dst_ref=shares_ref.at[origin, seq],
            send_sem=share_send.at[origin, target], recv_sem=share_recv.at[origin, seq],
            device_id=(target, head), device_id_type=MESH,
        )

    def send_share(origin):
        share_ref[origin] = (acc_ref[origin] * scale).astype(BF16)
        for target in range(reducers):
            @pl.when(seq != target)
            def _():
                share_copy(origin, target).start()

    def final_copy(origin, owner):
        columns = pl.ds(owner * piece if piece < width else 0, piece)
        return pltpu.make_async_remote_copy(
            src_ref=final_ref.at[origin, :, columns] if piece < width else final_ref.at[origin],
            dst_ref=finals_ref.at[pl.ds(pl.multiple_of(seq * rows_per, rows_per), rows_per), :],
            send_sem=final_send.at[origin, owner], recv_sem=final_recv.at[seq],
            device_id=(head * owners + owner, origin), device_id_type=MESH,
        )

    def is_self(origin, owner):
        return jnp.logical_and(head * owners + owner == seq, origin == head)

    def reduce_share(origin):
        @pl.when(seq < reducers)
        def _():
            mine = pl.ds(pl.multiple_of(seq * rows_per, rows_per), rows_per)
            final_ref[origin] = acc_ref[origin, mine, :] * scale

            def add(step, carry):
                source = lax.rem(seq + step, n_seq)
                pltpu.make_async_remote_copy(
                    src_ref=share_ref.at[origin, pl.ds(0, rows_per), :],
                    dst_ref=shares_ref.at[origin, source],
                    send_sem=share_send.at[origin, 0], recv_sem=share_recv.at[origin, source],
                    device_id=(source, head), device_id_type=MESH,
                ).wait_recv()
                final_ref[origin] += shares_ref[origin, source].astype(F32)
                return carry

            lax.fori_loop(1, n_seq, add, 0)
            for owner in range(owners):
                @pl.when(jnp.logical_not(is_self(origin, owner)))
                def _():
                    final_copy(origin, owner).start()

                @pl.when(is_self(origin, owner))
                def _():
                    whole = final_ref[origin]
                    start = owner * piece if piece < width else 0
                    finals_ref[mine, :] = whole[:, start : start + piece]

    loads[3].wait()
    for c in range(CHUNKS):
        multiply(head, c, c == 0)
    send_share(head)
    waiting = [head]
    for distance in range(1, n_head // 2 + 1):
        met = []
        for c in range(CHUNKS):
            for way in range(2):
                if distance <= reach(way, c):
                    origin = ring_arrival(way, distance, c)
                    if distance < reach(way, c):
                        ring_copy(way, distance, c).start()
                    side = way if 2 * distance < n_head else 0
                    multiply(origin, c, side not in met)
                    met.append(side)
        done = [lax.rem(head + n_head - distance, n_head)]
        if 2 * distance < n_head:
            done.append(lax.rem(head + distance, n_head))
        for origin in done:
            send_share(origin)
        for origin in waiting:
            reduce_share(origin)
        waiting = done
    for origin in waiting:
        reduce_share(origin)

    home = seq // owners
    for source in range(reducers):
        @pl.when(jnp.logical_not(jnp.logical_and(seq == source, head == home)))
        def _():
            pltpu.make_async_remote_copy(
                src_ref=final_ref.at[0, :, pl.ds(0, piece)] if piece < width else final_ref.at[0],
                dst_ref=finals_ref.at[pl.ds(source * rows_per, rows_per), :],
                send_sem=final_send.at[0, 0], recv_sem=final_recv.at[source],
                device_id=(source, home), device_id_type=MESH,
            ).wait_recv()
    if grad_ref.shape[1] == piece:
        grad_ref[...] = finals_ref[...]
    else:
        per = grad_ref.shape[1]
        for owner in range(owners):
            @pl.when(lax.rem(seq, owners) == owner)
            def _():
                grad_ref[...] = finals_ref[...][:, owner * per : (owner + 1) * per]

    for target in range(1, n_seq):
        @pl.when(seq < target)
        def _():
            state_copy(target).wait_send()
    for c in range(CHUNKS):
        for way in range(2):
            for distance in range(reach(way, c)):
                ring_copy(way, distance, c).wait_send()
    for origin in range(n_head):
        for target in range(reducers):
            @pl.when(seq != target)
            def _():
                share_copy(origin, target).wait_send()

        @pl.when(seq < reducers)
        def _():
            for owner in range(owners):
                @pl.when(jnp.logical_not(is_self(origin, owner)))
                def _():
                    final_copy(origin, owner).wait_send()
    attn_copy.wait()


def body(n_seq, n_head, queries, keys, values, level_ids, level_table, out_cotangent):
    block_len, head_dim = queries.shape
    width = out_cotangent.shape[1]
    per = width * n_head // n_seq
    piece = per if per % 128 == 0 else width
    seq_bits = n_seq.bit_length() - 1
    inner = (block_len // TILE).bit_length() - 1
    rows_per = max(16, head_dim // n_seq)
    reducers = head_dim // rows_per
    steps = max(1, n_head // 2)
    dma = pltpu.SemaphoreType.DMA
    vmem = pl.BlockSpec(memory_space=pltpu.VMEM)
    hbm = pl.BlockSpec(memory_space=pl.ANY)
    attn_out, grad = pl.pallas_call(
        functools.partial(kernel, n_seq, n_head),
        out_shape=(
            jax.ShapeDtypeStruct((block_len, head_dim), BF16),
            jax.ShapeDtypeStruct((head_dim, per), F32),
        ),
        in_specs=[hbm, hbm, hbm, vmem, vmem, hbm],
        out_specs=(hbm, vmem),
        scratch_shapes=[
            pltpu.VMEM((block_len, head_dim), BF16),
            pltpu.VMEM((block_len, head_dim), BF16),
            pltpu.VMEM((block_len, head_dim), BF16),
            pltpu.VMEM((block_len, width), BF16),
            pltpu.VMEM((TILE, TILE), jnp.int32),
            pltpu.VMEM((block_len, level_table.shape[1]), F32),
            pltpu.VMEM((block_len, head_dim), F32),
            pltpu.VMEM((block_len // TILE, head_dim, inner * head_dim), BF16),
            pltpu.VMEM((head_dim, head_dim), BF16),
            pltpu.VMEM((n_seq, head_dim, head_dim), BF16),
            pltpu.VMEM((2 * head_dim, seq_bits * head_dim), BF16),
            pltpu.VMEM((block_len, head_dim), BF16),
            pltpu.VMEM((n_head, CHUNKS, head_dim, block_len // CHUNKS), BF16),
            pltpu.VMEM((n_head, head_dim, width), F32),
            pltpu.VMEM((n_head, head_dim, width), BF16),
            pltpu.VMEM((n_head, n_seq, rows_per, width), BF16),
            pltpu.VMEM((n_head, rows_per, width), F32),
            pltpu.VMEM((head_dim, piece), F32),
            dma((4,)),
            dma((1,)),
            dma((n_seq,)),
            dma((n_seq,)),
            dma((2, steps, CHUNKS)),
            dma((2, steps, CHUNKS)),
            dma((n_head, reducers)),
            dma((n_head, n_seq)),
            dma((n_head, n_seq // n_head)),
            dma((reducers,)),
        ],
        compiler_params=pltpu.CompilerParams(
            collective_id=0, has_side_effects=True, vmem_limit_bytes=60 * 2**20
        ),
    )(queries, keys, values, level_ids[None, :], level_table, out_cotangent)
    return attn_out, grad.T


def solution(mesh):
    in_specs = (
        P("seq", "head"),
        P("seq", "head"),
        P("seq", "head"),
        P("seq"),
        P(),
        P("seq", "head"),
    )
    out_specs = (P("seq", "head"), P("seq", "head"))
    return jax.shard_map(
        functools.partial(body, mesh.shape["seq"], mesh.shape["head"]),
        mesh=mesh, in_specs=in_specs, out_specs=out_specs, check_vma=False,
    )
```

time: 211 us -> 65.3 us (0.31); the launches traced: 208 us -> 65 us
  waiting for transfers between devices: 150 us -> 0 us
  Pallas kernels: 0 us -> 59.4 us
  matrix products: 38.8 us -> 0 us
  between operations: 14.3 us -> 0.64 us
  local copies, waits for them, and re-layouts: 2.23 us -> 4.93 us
    all_gather x1 -> x0, waiting for transfers between devices: 109 us -> none  [body(): full_cotangent = lax.all_gather(out_cotangent, 'head', axis=1, tiled=True)]
    pallas_call x0 -> x1, Pallas kernels: none -> 59.4 us  [body(): pl.pallas_call(functools.partial(kernel, n_seq, n_head), out_shape=(jax.S...]
    dot_general x8 -> x0, matrix products: 38.8 us -> none  [the longest x4 29.2 us: body(): jnp.dot(mixed, values[:last], preferred_element_type=jnp.float32)]
    reduce_scatter x1 -> x0, waiting for transfers between devices: 35.9 us -> none  [body(): lax.psum_scatter(lax.dot_general(full_cotangent, attn_out, (((0,), (0,)),...]
    ppermute x3 -> x0, waiting for transfers between devices: 4.25 us -> none  [partner_2(): return lax.ppermute(value, axis, pairs)]
    unnamed x13 -> x3, local copies, waits for them, and re-layouts: 1.69 us -> 4.93 us
  transfers between devices with their start and end apart: 5 -> 0, of which waited for: 4 -> 0; matrix products, arithmetic and copies ran while one was open for 17% -> 0% of each run, Pallas kernels for 0% -> 0%
where the time goes in v1:
time: 65.3 us; the launch traced here: 65 us
  Pallas kernels  59.4 us (91%)
  local copies, waits for them, and re-layouts  4.93 us (8%)
    pallas_call x1, Pallas kernels, body(): pl.pallas_call(functools.partial(kernel, n_seq, n_head), out_shape=(jax.S...  59.4 us
    unnamed x3, local copies, waits for them, and re-layouts  4.93 us

profile of v1, /device:TPU:15, one launch (start us, length us, event | category | flops | bytes accessed | tf_op | source)
XLA Modules:
  0.0 65.0 jit_solution(2281325255243055548)
XLA Ops:
  0.6 1.4 %copy.8.table_ref = f32[64,15]{1,0:T(8,128)} copy(f32[64,15]{0,1:T(8,128)} %param.10) | data formatting | bytes 7680 | tf_op args[4]
  2.0 59.4 %shard_map.77 = (bf16[2048,128]{1,0:T(8,128)(2,1)}, f32[128,256]{1,0:T(8,128)}) custom-call(bf16[2048,128]{1,0:T(8,128)(2,1)} %q_hbm.1, bf16[2048,128]{1,0:T(8,128)(2,1)} %k_hbm.1, bf16[2048,128]{1,0:T(8,128)(2,1)} %v_hbm.1, s32[1,2048]{1,0:T(1,128)} %bitcast.3, f32[64,15]{1,0:T(8,128)} %copy.8.table_ref, bf16[2048,512]{1,0:T(8,128)(2,1)} %cot_hbm.1), custom_call_target="tpu_custom_call" | custom-call | tf_op jit(solution)/shard_map/pallas_call | solution.py:356
  61.4 1.7 %copy.9 = f32[256,128]{1,0:T(8,128)} copy(f32[256,128]{0,1:T(8,128)} %bitcast.2) | data formatting | bytes 262144
  63.1 1.9 %copy.11 = bf16[2048,128]{1,0:T(8,128)(2,1)} copy(bf16[2048,128]{1,0:T(8,128)(2,1)} %get-tuple-element.10) | data formatting | bytes 1048576

commit v2 on v1

--- a/solution.py
+++ b/solution.py
@@ -9,7 +9,8 @@
 
 EPSILON = 1e-06
 TILE = 128
-CHUNKS = 4
+CHUNKS = 8
+KEEP = 5
 MESH = pl.DeviceIdType.MESH
 F32 = jnp.float32
 BF16 = jnp.bfloat16
@@ -35,9 +36,9 @@
     attn_hbm, grad_ref,
     q_ref, k_ref, v_ref, cot_ref, levels_ref, coeff_ref, total_ref, sib_ref,
     state_ref, states_ref, flat_ref, attn_ref, gather_ref, acc_ref,
-    share_ref, shares_ref, final_ref, finals_ref,
+    share_ref, shares_ref, final_ref, finals_ref, help_ref,
     load_sem, out_sem, state_send, state_recv, ring_send, ring_recv,
-    share_send, share_recv, final_send, final_recv,
+    share_send, share_recv, final_send, final_recv, help_send, help_recv,
 ):
     seq, head = lax.axis_index("seq"), lax.axis_index("head")
     block_len, head_dim = q_ref.shape
@@ -51,7 +52,9 @@
     owners = n_seq // n_head
     rows_per = max(16, head_dim // n_seq)
     reducers = head_dim // rows_per
-    piece = finals_ref.shape[1]
+    piece = finals_ref.shape[2]
+    last = n_head - 1
+    keep = CHUNKS - help_ref.shape[0] if n_head >= 4 else CHUNKS
     scale = (block_len * n_seq) ** (-0.5)
 
     loads = [
@@ -81,7 +84,7 @@
     rest = table - high.astype(F32)
     mid = rest.astype(BF16)
     low = (rest - mid.astype(F32)).astype(BF16)
-    table3 = jnp.concatenate([high, mid, low], axis=0)
+    table3 = jnp.concatenate([high, mid, low], axis=1)
     levels_ref[...] = tile_levels(TILE)
 
     loads[0].wait()
@@ -112,13 +115,34 @@
         def _():
             state_copy(target).start()
 
+    right, left = lax.rem(head + 1, n_head), lax.rem(head + n_head - 1, n_head)
+    places = (head, last - head)
+
+    def limit(c):
+        return jnp.where(c < keep, last, last - 1)
+
+    def help_copy(way, c):
+        return pltpu.make_async_remote_copy(
+            src_ref=cot_hbm.at[pl.ds(c * chunk, chunk), :], dst_ref=help_ref.at[c - keep],
+            send_sem=help_send.at[c - keep], recv_sem=help_recv.at[c - keep],
+            device_id=(seq, left if way == 0 else right), device_id_type=MESH,
+        )
+
+    for way in range(2):
+        @pl.when(places[way] == last)
+        def _():
+            for c in range(keep, CHUNKS):
+                help_copy(way, c).start()
+
+    acc_ref[...] = jnp.zeros_like(acc_ref)
+
     loads[2].wait()
 
     def local_tile(i, carry):
         rows = pl.ds(pl.multiple_of(i * TILE, TILE), TILE)
-        row_ids = lax.broadcasted_iota(jnp.int32, (table.shape[0], TILE), 0)
+        row_ids = lax.broadcasted_iota(jnp.int32, (table.shape[1], TILE), 0)
         onehot = (row_ids == ids_ref[:, rows]).astype(F32).astype(BF16)
-        coeff = dot(jnp.concatenate([onehot] * 3, axis=0), table3, 0, 0)
+        coeff = dot(jnp.concatenate([onehot] * 3, axis=0), table3, 0, 1)
         coeff_ref[rows, :] = coeff
         levels = levels_ref[...]
         weights = jnp.zeros((TILE, TILE), F32)
@@ -160,13 +184,11 @@
         def _():
             flat_ref[:, columns] = jnp.zeros((2 * head_dim, head_dim), BF16)
 
-    right, left = lax.rem(head + 1, n_head), lax.rem(head + n_head - 1, n_head)
-
-    def reach(way, c):
-        return n_head // 2 if (c < CHUNKS // 2) == (way == 0) else (n_head - 1) // 2
+    def origin_of(way, distance):
+        return lax.rem(head + (n_head - distance if way == 0 else distance), n_head)
 
     def ring_copy(way, distance, c):
-        origin = lax.rem(head + (n_head - distance if way == 0 else distance), n_head)
+        origin = origin_of(way, distance)
         return pltpu.make_async_remote_copy(
             src_ref=gather_ref.at[origin, c], dst_ref=gather_ref.at[origin, c],
             send_sem=ring_send.at[way, distance, c], recv_sem=ring_recv.at[way, distance, c],
@@ -174,13 +196,12 @@
         )
 
     def ring_arrival(way, distance, c):
-        origin = lax.rem(head + (n_head - distance if way == 0 else distance), n_head)
-        pltpu.make_async_remote_copy(
+        origin = origin_of(way, distance)
+        return pltpu.make_async_remote_copy(
             src_ref=gather_ref.at[origin, c], dst_ref=gather_ref.at[origin, c],
             send_sem=ring_send.at[way, distance - 1, c], recv_sem=ring_recv.at[way, distance - 1, c],
             device_id=(seq, right if way == 0 else left), device_id_type=MESH,
-        ).wait_recv()
-        return origin
+        )
 
     def attn_tile(first):
         def one(i, carry):
@@ -202,18 +223,19 @@
     for c in range(CHUNKS):
         lax.fori_loop(0, chunk // TILE, attn_tile(c), 0, unroll=True)
         for way in range(2):
-            if reach(way, c) > 0:
+            @pl.when(places[way] + 1 <= limit(c))
+            def _():
                 ring_copy(way, 0, c).start()
 
     attn_copy = pltpu.make_async_copy(attn_ref, attn_hbm, out_sem.at[0])
     attn_copy.start()
 
-    def multiply(origin, c, fresh):
-        part = dot(gather_ref[origin, c], cot_ref[pl.ds(c * chunk, chunk), :], 1, 0)
-        if fresh:
-            acc_ref[origin] = part
-        else:
-            acc_ref[origin] += part
+    def multiply(origin, c):
+        rows = pl.ds(pl.multiple_of(c * chunk, chunk), chunk)
+        acc_ref[origin] += dot(gather_ref[origin, c], cot_ref[rows, :], 1, 0)
+
+    def multiply_help(origin, c):
+        acc_ref[n_head + origin] += dot(gather_ref[origin, c], help_ref[c - keep], 1, 0)
 
     def share_copy(origin, target):
         return pltpu.make_async_remote_copy(
@@ -230,113 +252,163 @@
             def _():
                 share_copy(origin, target).start()
 
-    def final_copy(origin, owner):
+    def final_copy(slot, block, origin, kind, owner):
         columns = pl.ds(owner * piece if piece < width else 0, piece)
         return pltpu.make_async_remote_copy(
-            src_ref=final_ref.at[origin, :, columns] if piece < width else final_ref.at[origin],
-            dst_ref=finals_ref.at[pl.ds(pl.multiple_of(seq * rows_per, rows_per), rows_per), :],
-            send_sem=final_send.at[origin, owner], recv_sem=final_recv.at[seq],
-            device_id=(head * owners + owner, origin), device_id_type=MESH,
-        )
-
-    def is_self(origin, owner):
-        return jnp.logical_and(head * owners + owner == seq, origin == head)
-
-    def reduce_share(origin):
+            src_ref=final_ref.at[slot, :, columns] if piece < width else final_ref.at[slot],
+            dst_ref=finals_ref.at[kind, pl.ds(pl.multiple_of(seq * rows_per, rows_per), rows_per), :],
+            send_sem=final_send.at[slot, owner], recv_sem=final_recv.at[kind, seq],
+            device_id=(block * owners + owner, origin), device_id_type=MESH,
+        )
+
+    def is_self(block, origin, owner):
+        return jnp.logical_and(block * owners + owner == seq, origin == head)
+
+    def reduce_share(slot, block, origin, kind):
         @pl.when(seq < reducers)
         def _():
             mine = pl.ds(pl.multiple_of(seq * rows_per, rows_per), rows_per)
-            final_ref[origin] = acc_ref[origin, mine, :] * scale
+            final_ref[slot] = acc_ref[slot, mine, :] * scale
 
             def add(step, carry):
                 source = lax.rem(seq + step, n_seq)
                 pltpu.make_async_remote_copy(
-                    src_ref=share_ref.at[origin, pl.ds(0, rows_per), :],
-                    dst_ref=shares_ref.at[origin, source],
-                    send_sem=share_send.at[origin, 0], recv_sem=share_recv.at[origin, source],
+                    src_ref=share_ref.at[slot, pl.ds(0, rows_per), :],
+                    dst_ref=shares_ref.at[slot, source],
+                    send_sem=share_send.at[slot, 0], recv_sem=share_recv.at[slot, source],
                     device_id=(source, head), device_id_type=MESH,
                 ).wait_recv()
-                final_ref[origin] += shares_ref[origin, source].astype(F32)
+                final_ref[slot] += shares_ref[slot, source].astype(F32)
                 return carry
 
             lax.fori_loop(1, n_seq, add, 0)
             for owner in range(owners):
-                @pl.when(jnp.logical_not(is_self(origin, owner)))
+                @pl.when(jnp.logical_not(is_self(block, origin, owner)))
                 def _():
-                    final_copy(origin, owner).start()
-
-                @pl.when(is_self(origin, owner))
+                    final_copy(slot, block, origin, kind, owner).start()
+
+                @pl.when(is_self(block, origin, owner))
                 def _():
-                    whole = final_ref[origin]
+                    whole = final_ref[slot]
                     start = owner * piece if piece < width else 0
-                    finals_ref[mine, :] = whole[:, start : start + piece]
+                    finals_ref[kind, mine, :] = whole[:, start : start + piece]
 
     loads[3].wait()
-    for c in range(CHUNKS):
-        multiply(head, c, c == 0)
+
+    def own_chunk(c, carry):
+        multiply(head, c)
+        return carry
+
+    lax.fori_loop(0, CHUNKS, own_chunk, 0)
     send_share(head)
-    waiting = [head]
-    for distance in range(1, n_head // 2 + 1):
-        met = []
-        for c in range(CHUNKS):
+    every = [(head >= 0, head, head, head, 0)]
+    waiting = list(every)
+    helps = n_head >= 4
+    for distance in range(1, n_head):
+        def arrivals(c, carry):
             for way in range(2):
-                if distance <= reach(way, c):
-                    origin = ring_arrival(way, distance, c)
-                    if distance < reach(way, c):
-                        ring_copy(way, distance, c).start()
-                    side = way if 2 * distance < n_head else 0
-                    multiply(origin, c, side not in met)
-                    met.append(side)
-        done = [lax.rem(head + n_head - distance, n_head)]
-        if 2 * distance < n_head:
-            done.append(lax.rem(head + distance, n_head))
-        for origin in done:
-            send_share(origin)
-        for origin in waiting:
-            reduce_share(origin)
+                place = places[way]
+
+                @pl.when(jnp.logical_and(place >= distance, place <= limit(c)))
+                def _():
+                    ring_arrival(way, distance, c).wait_recv()
+                    if distance < last:
+                        @pl.when(place + 1 <= limit(c))
+                        def _():
+                            ring_copy(way, distance, c).start()
+                    origin = origin_of(way, distance)
+                    multiply(origin, c)
+                    if helps and distance < last:
+                        @pl.when(jnp.logical_and(place == last - 1, c >= keep))
+                        def _():
+                            if distance == 1:
+                                help_copy(way, c).wait_recv()
+                                multiply_help(head, c)
+                            multiply_help(origin, c)
+            return carry
+
+        lax.fori_loop(0, CHUNKS, arrivals, 0)
+        done = []
+        for way in range(2):
+            origin, place = origin_of(way, distance), places[way]
+            done.append((place >= distance, origin, head, origin, 0))
+            if helps and distance < last:
+                block = last if way == 0 else 0
+                helper = place == last - 1
+                if distance == 1:
+                    done.append((helper, n_head + head, block, head, 1))
+                done.append((helper, n_head + origin, block, origin, 1))
+        for condition, slot, _, _, _ in done:
+            pl.when(condition)(functools.partial(send_share, slot))
+        for condition, *rest in waiting:
+            pl.when(condition)(functools.partial(reduce_share, *rest))
+        every += done
         waiting = done
-    for origin in waiting:
-        reduce_share(origin)
+    for condition, *rest in waiting:
+        pl.when(condition)(functools.partial(reduce_share, *rest))
 
     home = seq // owners
-    for source in range(reducers):
-        @pl.when(jnp.logical_not(jnp.logical_and(seq == source, head == home)))
-        def _():
-            pltpu.make_async_remote_copy(
-                src_ref=final_ref.at[0, :, pl.ds(0, piece)] if piece < width else final_ref.at[0],
-                dst_ref=finals_ref.at[pl.ds(source * rows_per, rows_per), :],
-                send_sem=final_send.at[0, 0], recv_sem=final_recv.at[source],
-                device_id=(source, home), device_id_type=MESH,
-            ).wait_recv()
-    if grad_ref.shape[1] == piece:
-        grad_ref[...] = finals_ref[...]
+    at_end = jnp.logical_and(jnp.logical_or(home == 0, home == last), head != home)
+    for kind in range(2 if helps else 1):
+        plane = home if kind == 0 else jnp.where(home == 0, 1, last - 1)
+        for source in range(reducers):
+            away = jnp.logical_not(jnp.logical_and(seq == source, head == plane))
+
+            @pl.when(jnp.logical_and(away, at_end) if kind else away)
+            def _():
+                pltpu.make_async_remote_copy(
+                    src_ref=final_ref.at[0, :, pl.ds(0, piece)] if piece < width else final_ref.at[0],
+                    dst_ref=finals_ref.at[kind, pl.ds(source * rows_per, rows_per), :],
+                    send_sem=final_send.at[0, 0], recv_sem=final_recv.at[kind, source],
+                    device_id=(source, plane), device_id_type=MESH,
+                ).wait_recv()
+    if helps:
+        @pl.when(at_end)
+        def _():
+            finals_ref[0] += finals_ref[1]
+    per = grad_ref.shape[1]
+    if per == piece:
+        grad_ref[...] = finals_ref[0]
     else:
-        per = grad_ref.shape[1]
         for owner in range(owners):
             @pl.when(lax.rem(seq, owners) == owner)
             def _():
-                grad_ref[...] = finals_ref[...][:, owner * per : (owner + 1) * per]
+                grad_ref[...] = finals_ref[0][:, owner * per : (owner + 1) * per]
 
     for target in range(1, n_seq):
         @pl.when(seq < target)
         def _():
             state_copy(target).wait_send()
-    for c in range(CHUNKS):
-        for way in range(2):
-            for distance in range(reach(way, c)):
-                ring_copy(way, distance, c).wait_send()
-    for origin in range(n_head):
-        for target in range(reducers):
-            @pl.when(seq != target)
+    for way in range(2):
+        place = places[way]
+
+        @pl.when(place == last)
+        def _():
+            for c in range(keep, CHUNKS):
+                help_copy(way, c).wait_send()
+
+        for distance in range(last):
+            def drain(c, carry):
+                @pl.when(jnp.logical_and(place >= distance, place + 1 <= limit(c)))
+                def _():
+                    ring_copy(way, distance, c).wait_send()
+                return carry
+
+            lax.fori_loop(0, CHUNKS, drain, 0)
+    for condition, slot, block, origin, kind in every:
+        @pl.when(condition)
+        def _():
+            for target in range(reducers):
+                @pl.when(seq != target)
+                def _():
+                    share_copy(slot, target).wait_send()
+
+            @pl.when(seq < reducers)
             def _():
-                share_copy(origin, target).wait_send()
-
-        @pl.when(seq < reducers)
-        def _():
-            for owner in range(owners):
-                @pl.when(jnp.logical_not(is_self(origin, owner)))
-                def _():
-                    final_copy(origin, owner).wait_send()
+                for owner in range(owners):
+                    @pl.when(jnp.logical_not(is_self(block, origin, owner)))
+                    def _():
+                        final_copy(slot, block, origin, kind, owner).wait_send()
     attn_copy.wait()
 
 
@@ -349,7 +421,8 @@
     inner = (block_len // TILE).bit_length() - 1
     rows_per = max(16, head_dim // n_seq)
     reducers = head_dim // rows_per
-    steps = max(1, n_head // 2)
+    steps = max(1, n_head - 1)
+    slots = 2 * n_head
     dma = pltpu.SemaphoreType.DMA
     vmem = pl.BlockSpec(memory_space=pltpu.VMEM)
     hbm = pl.BlockSpec(memory_space=pl.ANY)
@@ -375,26 +448,29 @@
             pltpu.VMEM((2 * head_dim, seq_bits * head_dim), BF16),
             pltpu.VMEM((block_len, head_dim), BF16),
             pltpu.VMEM((n_head, CHUNKS, head_dim, block_len // CHUNKS), BF16),
-            pltpu.VMEM((n_head, head_dim, width), F32),
-            pltpu.VMEM((n_head, head_dim, width), BF16),
-            pltpu.VMEM((n_head, n_seq, rows_per, width), BF16),
-            pltpu.VMEM((n_head, rows_per, width), F32),
-            pltpu.VMEM((head_dim, piece), F32),
+            pltpu.VMEM((slots, head_dim, width), F32),
+            pltpu.VMEM((slots, head_dim, width), BF16),
+            pltpu.VMEM((slots, n_seq, rows_per, width), BF16),
+            pltpu.VMEM((slots, rows_per, width), F32),
+            pltpu.VMEM((2, head_dim, piece), F32),
+            pltpu.VMEM((CHUNKS - KEEP, block_len // CHUNKS, width), BF16),
             dma((4,)),
             dma((1,)),
             dma((n_seq,)),
             dma((n_seq,)),
             dma((2, steps, CHUNKS)),
             dma((2, steps, CHUNKS)),
-            dma((n_head, reducers)),
-            dma((n_head, n_seq)),
-            dma((n_head, n_seq // n_head)),
-            dma((reducers,)),
+            dma((slots, reducers)),
+            dma((slots, n_seq)),
+            dma((slots, n_seq // n_head)),
+            dma((2, reducers)),
+            dma((CHUNKS - KEEP,)),
+            dma((CHUNKS - KEEP,)),
         ],
         compiler_params=pltpu.CompilerParams(
             collective_id=0, has_side_effects=True, vmem_limit_bytes=60 * 2**20
         ),
-    )(queries, keys, values, level_ids[None, :], level_table, out_cotangent)
+    )(queries, keys, values, level_ids[None, :], level_table.T, out_cotangent)
     return attn_out, grad.T
 
 

time: 65.3 us -> 62.5 us (0.957)
  the two profiles are of different devices: /device:TPU:15 before, /device:TPU:25 now
where the time goes in v2:
time: 62.5 us; the launch traced here: 62.2 us
  Pallas kernels  58.1 us (93%)
  local copies, waits for them, and re-layouts  3.53 us (6%)
  between operations  0.64 us (1%)
    pallas_call x1, Pallas kernels, body(): pl.pallas_call(functools.partial(kernel, n_seq, n_head), out_shape=(jax.S...  58.1 us
    unnamed x2, local copies, waits for them, and re-layouts  3.53 us

profile of v2, /device:TPU:25, one launch (start us, length us, event | category | flops | bytes accessed | tf_op | source)
XLA Modules:
  0.0 62.2 jit_solution(14245332560567421234)
XLA Ops:
  0.6 58.1 %shard_map.77 = (bf16[2048,128]{1,0:T(8,128)(2,1)}, f32[128,256]{1,0:T(8,128)}) custom-call(bf16[2048,128]{1,0:T(8,128)(2,1)} %q_hbm.1, bf16[2048,128]{1,0:T(8,128)(2,1)} %k_hbm.1, bf16[2048,128]{1,0:T(8,128)(2,1)} %v_hbm.1, s32[1,2048]{1,0:T(1,128)} %bitcast.4, f32[15,64]{1,0:T(8,128)} %bitcast.5, bf16[2048,512]{1,0:T(8,128)(2,1)} %cot_hbm.1), custom_call_target="tpu_custom_call" | custom-call | tf_op jit(solution)/shard_map/pallas_call | solution.py:429
  58.7 1.7 %copy.8 = f32[256,128]{1,0:T(8,128)} copy(f32[256,128]{0,1:T(8,128)} %bitcast.3) | data formatting | bytes 262144
  60.4 1.9 %copy.10 = bf16[2048,128]{1,0:T(8,128)(2,1)} copy(bf16[2048,128]{1,0:T(8,128)(2,1)} %get-tuple-element.10) | data formatting | bytes 1048576
